TPU v7x, 256 devices: a whole 4x4x8 slice. The times are simulated.
256 devices in a mesh: fsdp: 32 (over z_hi, y, core), tensor: 8 (over z_lo, x).
Axes of the slice: x: 4, y: 4, z: 8 (z_hi: 4, z_lo: 2; z = z_hi * 2 + z_lo), core: 2. Of those that a mesh axis runs over, the one named last changes fastest.
Arguments:
- tokens: bfloat16 [4096, 8192], P('fsdp'), may hold values from -6 to 6
- cotangent: bfloat16 [4096, 8192], P('fsdp'), may hold values from -1.5 to 1.5
- gate_blocks: bfloat16 [8, 64, 128, 128], P('tensor', 'fsdp'), may hold values from -0.25 to 0.25
- up_blocks: bfloat16 [8, 64, 128, 128], P('tensor', 'fsdp'), may hold values from -0.25 to 0.25
- down_blocks: bfloat16 [8, 64, 128, 128], P('tensor', 'fsdp'), may hold values from -0.25 to 0.25
- gate_where: int32 [8, 64], P('tensor'), may hold values from 0 to 895, as said below
- up_where: int32 [8, 64], P('tensor'), may hold values from 0 to 895, as said below
- down_where: int32 [8, 64], P('tensor'), may hold values from 0 to 895, as said below
- block_counts: int32 [3, 8], P(None, 'tensor'), may hold values from 32 to 64, as said below
Outputs:
- outputs: bfloat16 [4096, 8192], P('fsdp', 'tensor')
- input_grads: bfloat16 [4096, 8192], P('fsdp', 'tensor')
- gate_grads: bfloat16 [8, 64, 128, 128], P('tensor', 'fsdp')
- up_grads: bfloat16 [8, 64, 128, 128], P('tensor', 'fsdp')
- down_grads: bfloat16 [8, 64, 128, 128], P('tensor', 'fsdp')
Inputs may be any that keep to these rules, and one draw needn't show every extreme that they name: Within one group of hidden units the 64 positions of gate_where are distinct. Within one group of hidden units the 64 positions of up_where are distinct. Within one group of hidden units the 64 positions of down_where are distinct. `block_counts`: for each matrix some group has all 64 slots live.
All inputs are finite; a program needn't handle non-finite values.
Results may differ from a plain program's by a relative error of at most 0.015.
Values may be sent and summed in bfloat16 or wider, within the bound.
A program may use at most 128 MiB of HBM per device.

v0:
```python
import jax
import jax.numpy as jnp
from jax import lax
from jax.sharding import PartitionSpec as P

FF = 14336


def blockwise(pattern, left_side, right_side):
    return jnp.einsum(pattern, left_side, right_side, preferred_element_type=jnp.float32)


def collect(block_terms, segment_ids, segments):
    return jax.ops.segment_sum(block_terms, segment_ids, num_segments=segments)


def shards(
    tokens,
    cotangent,
    gate_blocks,
    up_blocks,
    down_blocks,
    gate_where,
    up_where,
    down_where,
    block_counts,
):
    tok_rows, tok_width = tokens.shape
    row_blocks = tok_width // 128
    col_blocks = FF // (128 * lax.axis_size("tensor"))
    slot_count = gate_where.shape[1]
    rows_blocked = tokens.reshape(tok_rows, row_blocks, 128).transpose(1, 0, 2)
    grad_blocked = cotangent.reshape(tok_rows, row_blocks, 128).transpose(1, 0, 2)
    live_slots = lax.broadcasted_iota(jnp.int32, (3, slot_count), 1) < block_counts
    live_blocks = live_slots.astype(jnp.bfloat16)[:, :, None, None]
    live_parts = live_slots.astype(jnp.float32)[:, :, None, None]
    gate_all, up_all, down_all = (
        lax.all_gather(gate_blocks, "fsdp", axis=1, tiled=True),
        lax.all_gather(up_blocks, "fsdp", axis=1, tiled=True),
        lax.all_gather(down_blocks, "fsdp", axis=1, tiled=True),
    )
    gate_eff = gate_all[0] * live_blocks[0]
    up_eff = up_all[0] * live_blocks[1]
    gate_row = gate_where[0] // col_blocks
    gate_col = gate_where[0] % col_blocks
    up_row = up_where[0] // col_blocks
    up_col = up_where[0] % col_blocks
    down_ff = down_where[0] // row_blocks
    down_d = down_where[0] % row_blocks
    rows_gate = jnp.take(rows_blocked, gate_row, axis=0)
    rows_up = jnp.take(rows_blocked, up_row, axis=0)
    gate_val = collect(blockwise("ntk,nkj->ntj", rows_gate, gate_eff), gate_col, col_blocks)
    up_val = collect(blockwise("ntk,nkj->ntj", rows_up, up_eff), up_col, col_blocks)
    down_eff = down_all[0] * live_blocks[2]
    gate_sig = jax.nn.sigmoid(gate_val)
    silu_gate = gate_val * gate_sig
    hidden = (silu_gate * up_val).astype(jnp.bfloat16)
    hidden_sel = jnp.take(hidden, down_ff, axis=0)
    grad_sel = jnp.take(grad_blocked, down_d, axis=0)
    output_term = collect(blockwise("ntk,nkj->ntj", hidden_sel, down_eff), down_d, row_blocks)
    output_sum = lax.psum_scatter(
        output_term.astype(jnp.bfloat16), "tensor", scatter_dimension=0, tiled=True
    ).astype(jnp.float32)
    hidden_grad = collect(blockwise("ntj,nkj->ntk", grad_sel, down_eff), down_ff, col_blocks)
    down_part = blockwise("ntk,ntj->nkj", hidden_sel, grad_sel) * live_parts[2]
    gate_delta = (hidden_grad * up_val * gate_sig * (1.0 + gate_val * (1.0 - gate_sig))).astype(
        jnp.bfloat16
    )
    up_delta = (hidden_grad * silu_gate).astype(jnp.bfloat16)
    delta_gate = jnp.take(gate_delta, gate_col, axis=0)
    delta_up = jnp.take(up_delta, up_col, axis=0)
    input_term = collect(blockwise("ntj,nkj->ntk", delta_gate, gate_eff), gate_row, row_blocks)
    input_term = input_term + collect(
        blockwise("ntj,nkj->ntk", delta_up, up_eff), up_row, row_blocks
    )
    gate_part = blockwise("ntk,ntj->nkj", rows_gate, delta_gate) * live_parts[0]
    up_part = blockwise("ntk,ntj->nkj", rows_up, delta_up) * live_parts[1]
    gate_sum, up_sum, down_sum = (
        lax.psum_scatter(
            gate_part[None].astype(jnp.bfloat16), "fsdp", scatter_dimension=1, tiled=True
        ).astype(jnp.float32),
        lax.psum_scatter(
            up_part[None].astype(jnp.bfloat16), "fsdp", scatter_dimension=1, tiled=True
        ).astype(jnp.float32),
        lax.psum_scatter(
            down_part[None].astype(jnp.bfloat16), "fsdp", scatter_dimension=1, tiled=True
        ).astype(jnp.float32),
    )
    input_sum = lax.psum_scatter(
        input_term.astype(jnp.bfloat16), "tensor", scatter_dimension=0, tiled=True
    ).astype(jnp.float32)
    outputs = output_sum.transpose(1, 0, 2).reshape(tok_rows, -1).astype(jnp.bfloat16)
    input_grads = input_sum.transpose(1, 0, 2).reshape(tok_rows, -1).astype(jnp.bfloat16)
    return (
        outputs,
        input_grads,
        gate_sum.astype(jnp.bfloat16),
        up_sum.astype(jnp.bfloat16),
        down_sum.astype(jnp.bfloat16),
    )


def solution(mesh):
    placed = (
        P("fsdp", None),
        P("fsdp", None),
        P("tensor", "fsdp", None, None),
        P("tensor", "fsdp", None, None),
        P("tensor", "fsdp", None, None),
        P("tensor", None),
        P("tensor", None),
        P("tensor", None),
        P(None, "tensor"),
    )
    return jax.shard_map(
        shards,
        mesh=mesh,
        in_specs=placed,
        out_specs=(
            P("fsdp", "tensor"),
            P("fsdp", "tensor"),
            P("tensor", "fsdp", None, None),
            P("tensor", "fsdp", None, None),
            P("tensor", "fsdp", None, None),
        ),
        check_vma=False,
    )
```

profile of v0, /device:TPU:2, one launch (start us, length us, event | category | flops | bytes accessed | tf_op | source)
XLA Modules:
  0.0 606.7 jit_solution(10214975213814710242)
XLA Ops:
  7.9 0.7 all-gather.4.cloned.1.call-update
  8.7 0.7 all-gather.6.cloned.1.call-update
  9.4 4.1 copy.31
  13.6 3.2 copy.32
  16.9 2.2 gather_fusion.1
  19.1 2.2 gather_fusion
  21.3 3.2 copy.37
  24.5 3.0 copy.38
  27.5 2.5 gather_fusion.3
  30.2 38.1 %all-gather.8.cloned.1.call-done = bf16[1,64,128,128]{3,2,0,1:T(8,128)(2,1)} async-done(((bf16[1,2,128,128]{3,2,0,1:T(8,128)(2,1)}), bf16[1,64,128,128]{3,2,0,1:T(8,128)(2,1)}) %all-gather.8.cloned.1.call-update) | async-done | bytes 2097168 | tf_op jit(solution)/shard_map/all_gather | solution.py:40
  68.3 5.2 fusion.4
  73.6 8.9 %scatter_fusion.3 = f32[14,128,128]{2,1,0:T(8,128)S(1)} fusion(f32[14,128,128]{2,1,0:T(8,128)S(1)} %broadcast.235.clone, s32[64]{0:T(128)S(1)} %get-tuple-element.50, f32[64,128,128]{2,1,0:T(8,128)} %fusion.4), kind=kCustom, calls=%fused_computation.9 | custom fusion | flops 1048576 | bytes 12583168 | tf_op jit(solution)/shard_map/scatter-add | solution.py:14
  82.5 40.1 %all-gather.4.cloned.1.call-done = bf16[1,64,128,128]{3,2,0,1:T(8,128)(2,1)} async-done(((bf16[1,2,128,128]{3,2,0,1:T(8,128)(2,1)}), bf16[1,64,128,128]{3,2,0,1:T(8,128)(2,1)}) %all-gather.4.cloned.1.call-update) | async-done | bytes 2097168 | tf_op jit(solution)/shard_map/all_gather | solution.py:38
  122.7 4.3 fusion.1
  127.1 8.8 %scatter_fusion = f32[14,128,128]{2,1,0:T(8,128)S(1)} fusion(f32[14,128,128]{2,1,0:T(8,128)S(1)} %broadcast.235.clone.1, s32[64]{0:T(128)S(1)} %get-tuple-element.52, f32[64,128,128]{2,1,0:T(8,128)} %fusion.1), kind=kCustom, calls=%fused_computation.6 | custom fusion | flops 1048576 | bytes 12583168 | tf_op jit(solution)/shard_map/scatter-add | solution.py:14
  135.9 41.1 %all-gather.6.cloned.1.call-done = bf16[1,64,128,128]{3,2,0,1:T(8,128)(2,1)} async-done(((bf16[1,2,128,128]{3,2,0,1:T(8,128)(2,1)}), bf16[1,64,128,128]{3,2,0,1:T(8,128)(2,1)}) %all-gather.6.cloned.1.call-update) | async-done | bytes 2097168 | tf_op jit(solution)/shard_map/all_gather | solution.py:39
  177.0 5.0 fusion.3
  182.0 8.8 %scatter_fusion.1 = f32[14,128,128]{2,1,0:T(8,128)S(1)} fusion(f32[14,128,128]{2,1,0:T(8,128)S(1)} %broadcast.235.clone.2, s32[64]{0:T(128)S(1)} %get-tuple-element.53, f32[64,128,128]{2,1,0:T(8,128)} %fusion.3), kind=kCustom, calls=%fused_computation.7 | custom fusion | flops 1048576 | bytes 12583168 | tf_op jit(solution)/shard_map/scatter-add | solution.py:14
  190.8 1.6 multiply_convert_fusion.3
  192.5 3.3 gather_fusion.2
  195.8 4.3 fusion.5
  200.1 2.5 broadcast.233.clone
  202.6 13.5 %scatter_fusion.2 = f32[64,128,128]{2,1,0:T(8,128)} fusion(f32[64,128,128]{2,1,0:T(8,128)} %broadcast.233.clone, s32[64]{0:T(128)S(1)} %get-tuple-element.51, f32[64,128,128]{2,1,0:T(8,128)} %fusion.5), kind=kCustom, calls=%fused_computation.8 | custom fusion | flops 1048576 | bytes 12583168 | tf_op jit(solution)/shard_map/scatter-add | solution.py:14
  216.1 3.9 convert_element_type.63
  220.3 0.8 copy-done
  221.1 2.2 gather_fusion.5
  223.3 2.2 gather_fusion.4
  225.4 5.2 fusion
  230.6 2.5 broadcast.233.clone.1
  233.1 13.7 %scatter_fusion.4 = f32[64,128,128]{2,1,0:T(8,128)} fusion(f32[64,128,128]{2,1,0:T(8,128)} %broadcast.233.clone.1, s32[64]{0:T(128)S(1)} %get-tuple-element.25, f32[64,128,128]{2,1,0:T(8,128)} %fusion), kind=kCustom, calls=%fused_computation.10 | custom fusion | flops 1048576 | bytes 12583168 | tf_op jit(solution)/shard_map/scatter-add | solution.py:14
  246.8 5.2 fusion.2
  252.1 2.5 broadcast.233.clone.2
  254.5 13.6 %scatter_fusion.5 = f32[64,128,128]{2,1,0:T(8,128)} fusion(f32[64,128,128]{2,1,0:T(8,128)} %broadcast.233.clone.2, s32[64]{0:T(128)S(1)} %get-tuple-element.19, f32[64,128,128]{2,1,0:T(8,128)} %fusion.2), kind=kCustom, calls=%fused_computation.11 | custom fusion | flops 1048576 | bytes 12583168 | tf_op jit(solution)/shard_map/scatter-add | solution.py:14
  268.1 5.8 add_convert_fusion
  274.0 1.5 copy-done.4
  275.5 4.2 fusion.7
  279.7 1.5 copy-done.8
  281.2 4.4 fusion.6
  285.7 1.5 copy-done.6
  287.2 4.2 fusion.8
  291.4 1.1 copy.36
  292.5 0.9 copy.43
  293.4 20.3 %reduce-scatter.8.cloned.1.call-done = bf16[8,128,128]{2,1,0:T(8,128)(2,1)} async-done(((bf16[64,128,128]{2,1,0:T(8,128)(2,1)}), bf16[8,128,128]{2,1,0:T(8,128)(2,1)}) %reduce-scatter.8.cloned.1.call-update) | async-done | bytes 262160 | tf_op jit(solution)/shard_map/reduce_scatter | solution.py:89
  313.7 1.1 copy.39
  314.8 0.9 copy.44
  315.7 95.9 %reduce-scatter.12.cloned.1.call-done = bf16[1,2,128,128]{3,2,1,0:T(8,128)(2,1)} async-done(((bf16[1,64,128,128]{3,2,1,0:T(8,128)(2,1)}), bf16[1,2,128,128]{3,2,1,0:T(8,128)(2,1)}) %reduce-scatter.12.cloned.1.call-update) | async-done | bytes 65552 | tf_op jit(solution)/shard_map/reduce_scatter | solution.py:82
  411.6 94.2 %reduce-scatter.10.cloned.1.call-done = bf16[1,2,128,128]{3,2,1,0:T(8,128)(2,1)} async-done(((bf16[1,64,128,128]{3,2,1,0:T(8,128)(2,1)}), bf16[1,2,128,128]{3,2,1,0:T(8,128)(2,1)}) %reduce-scatter.10.cloned.1.call-update) | async-done | bytes 65552 | tf_op jit(solution)/shard_map/reduce_scatter | solution.py:79
  505.8 94.1 %reduce-scatter.14.cloned.1.call-done = bf16[1,2,128,128]{3,2,1,0:T(8,128)(2,1)} async-done(((bf16[1,64,128,128]{3,2,1,0:T(8,128)(2,1)}), bf16[1,2,128,128]{3,2,1,0:T(8,128)(2,1)}) %reduce-scatter.14.cloned.1.call-update) | async-done | bytes 65552 | tf_op jit(solution)/shard_map/reduce_scatter | solution.py:85
  (52 shorter events, 1.8 us)
Async XLA Ops:
  7.2 61.1 %all-gather.8.cloned.1.call-start = ((), (), s32[]{:S(2)}) async-start(), calls=%async_computation.7 | async-start | bytes 2162688 | tf_op jit(solution)/shard_map/all_gather | solution.py:40
  7.9 114.8 %all-gather.4.cloned.1.call-start = ((), (), s32[]{:S(2)}) async-start(), calls=%async_computation.5 | async-start | bytes 2162688 | tf_op jit(solution)/shard_map/all_gather | solution.py:38
  8.6 168.3 %all-gather.6.cloned.1.call-start = ((), (), s32[]{:S(2)}) async-start(), calls=%async_computation.6 | async-start | bytes 2162688 | tf_op jit(solution)/shard_map/all_gather | solution.py:39
  9.4 282.0 %reduce-scatter.6.cloned.1.call-start = ((), (), s32[]{:S(2)}) async-start(), calls=%async_computation.8 | async-start | bytes 2359296 | tf_op jit(solution)/shard_map/reduce_scatter | solution.py:61
  13.6 3.2 copy-start.9
  16.9 2.2 copy-start.10
  24.5 3.0 copy-start.11
  27.5 2.6 copy-start.12
  30.1 43.4 %copy-start.5 = (bf16[64,128,128]{2,1,0:T(8,128)(2,1)}, bf16[64,128,128]{2,1,0:T(8,128)(2,1)S(1)}, u32[]{:S(2)}) copy-start(bf16[64,128,128]{2,1,0:T(8,128)(2,1)S(1)} %gather_fusion.3) | copy-start | bytes 6291460
  73.6 49.1 %copy-start.7 = (bf16[64,128,128]{2,1,0:T(8,128)(2,1)S(1)}, bf16[64,128,128]{2,1,0:T(8,128)(2,1)}, u32[]{:S(2)}) copy-start(bf16[64,128,128]{2,1,0:T(8,128)(2,1)} %gather_fusion) | copy-start | bytes 6291460
  192.5 3.3 copy-start.3
  220.0 1.0 copy-start
  220.1 93.6 %reduce-scatter.8.cloned.1.call-start = ((), (), s32[]{:S(2)}) async-start(), calls=%async_computation.9 | async-start | bytes 2359296 | tf_op jit(solution)/shard_map/reduce_scatter | solution.py:89
  223.3 2.2 copy-start.1
  233.1 13.7 %copy-start.2 = (bf16[1,64,128,128]{3,2,0,1:T(8,128)(2,1)S(1)}, bf16[1,64,128,128]{3,2,0,1:T(8,128)(2,1)}, u32[]{:S(2)}) copy-start(bf16[1,64,128,128]{3,2,0,1:T(8,128)(2,1)} %all-gather.6.cloned.1.call-done) | copy-start | bytes 6291460
  273.9 1.6 copy-start.4
  273.9 137.7 %reduce-scatter.12.cloned.1.call-start = ((), (), s32[]{:S(2)}) async-start(), calls=%async_computation.11 | async-start | bytes 2162688 | tf_op jit(solution)/shard_map/reduce_scatter | solution.py:82
  279.6 1.6 copy-start.8
  279.7 226.1 %reduce-scatter.10.cloned.1.call-start = ((), (), s32[]{:S(2)}) async-start(), calls=%async_computation.10 | async-start | bytes 2162688 | tf_op jit(solution)/shard_map/reduce_scatter | solution.py:79
  285.6 1.6 copy-start.6
  285.6 314.3 %reduce-scatter.14.cloned.1.call-start = ((), (), s32[]{:S(2)}) async-start(), calls=%async_computation.12 | async-start | bytes 2162688 | tf_op jit(solution)/shard_map/reduce_scatter | solution.py:85
Sparse Core Ops, SparseCore 0:
  10.5 57.7 all-gather.7
  70.9 51.7 all-gather.3
  125.2 51.7 all-gather.5
  220.2 39.8 reduce-scatter.5
  274.0 39.6 reduce-scatter.7
  318.0 93.5 reduce-scatter.11
  416.0 89.6 reduce-scatter.9
  510.2 89.6 reduce-scatter.13
where the time goes:
time: 608 us; the launch traced here: 607 us
  waiting for transfers between devices  426 us (70%)
  other arithmetic  78.8 us (13%)
  local copies, waits for them, and re-layouts  45.1 us (7%)
  matrix products  42 us (7%)
  between operations  14.4 us (2%)
    reduce_scatter x1, waiting for transfers between devices, shards(): lax.psum_scatter(up_part[None].astype(jnp.bfloat16), 'fsdp', scatter_dime...  95.9 us
    reduce_scatter x1, waiting for transfers between devices, shards(): lax.psum_scatter(gate_part[None].astype(jnp.bfloat16), 'fsdp', scatter_di...  94.2 us
    reduce_scatter x1, waiting for transfers between devices, shards(): lax.psum_scatter(down_part[None].astype(jnp.bfloat16), 'fsdp', scatter_di...  94.1 us
    scatter-add x6, other arithmetic, collect(): return jax.ops.segment_sum(block_terms, segment_ids, num_segments=segments)  67.3 us
    dot_general x9, matrix products, blockwise(): jnp.einsum(pattern, left_side, right_side, preferred_element_type=jnp.flo...  42 us
    all_gather x1, waiting for transfers between devices, shards(): lax.all_gather(up_blocks, 'fsdp', axis=1, tiled=True)  41.1 us
    all_gather x1, waiting for transfers between devices, shards(): lax.all_gather(gate_blocks, 'fsdp', axis=1, tiled=True)  40.1 us
    all_gather x1, waiting for transfers between devices, shards(): lax.all_gather(down_blocks, 'fsdp', axis=1, tiled=True)  38.1 us
  transfers between devices with their start and end apart: 8, of which 7 were waited for; matrix products, arithmetic and copies ran while one was open for 19% of the time, Pallas kernels for 0%

commit v1 on v0

--- a/solution.py
+++ b/solution.py
@@ -37,7 +37,9 @@
     gate_all, up_all, down_all = (
         lax.all_gather(gate_blocks, "fsdp", axis=1, tiled=True),
         lax.all_gather(up_blocks, "fsdp", axis=1, tiled=True),
-        lax.all_gather(down_blocks, "fsdp", axis=1, tiled=True),
+        jnp.concatenate(
+            lax.all_to_all(jnp.stack([down_blocks] * lax.axis_size("fsdp")), "fsdp", 0, 0), axis=1
+        ),
     )
     gate_eff = gate_all[0] * live_blocks[0]
     up_eff = up_all[0] * live_blocks[1]

time: 608 us -> 572 us (0.941)
  waiting for transfers between devices: 426 us -> 375 us
  starting transfers between devices: 0.5 us -> 12.2 us
    all_gather x1, waiting for transfers between devices: 40.1 us -> 0.02 us  [shards(): lax.all_gather(gate_blocks, 'fsdp', axis=1, tiled=True)]
    all_to_all x0 -> x1, waiting for transfers between devices: none -> 40 us  [shards(): lax.all_to_all(jnp.stack([down_blocks] * lax.axis_size('fsdp')), 'fsdp',...]
    all_gather x1 -> x0, waiting for transfers between devices: 38.1 us -> none  [shards(): lax.all_gather(down_blocks, 'fsdp', axis=1, tiled=True)]
    all_to_all x0 -> x1, starting transfers between devices: none -> 11.7 us  [shards(): lax.all_to_all(jnp.stack([down_blocks] * lax.axis_size('fsdp')), 'fsdp',...]
    all_gather x1, waiting for transfers between devices: 41.1 us -> 29.4 us  [shards(): lax.all_gather(up_blocks, 'fsdp', axis=1, tiled=True)]
    unnamed x30 -> x34, local copies, waits for them, and re-layouts: 14.4 us -> 13.9 us
  transfers between devices with their start and end apart: 8 -> 8, of which waited for: 7 -> 6; matrix products, arithmetic and copies ran while one was open for 19% -> 21% of each run, Pallas kernels for 0% -> 0%
where the time goes in v1:
time: 572 us; the launch traced here: 570 us
  waiting for transfers between devices  375 us (66%)
  other arithmetic  81 us (14%)
  local copies, waits for them, and re-layouts  47.1 us (8%)
  matrix products  40.4 us (7%)
  between operations  14.4 us (3%)
  starting transfers between devices  12.2 us (2%)
    reduce_scatter x1, waiting for transfers between devices, shards(): lax.psum_scatter(up_part[None].astype(jnp.bfloat16), 'fsdp', scatter_dime...  95.9 us
    reduce_scatter x1, waiting for transfers between devices, shards(): lax.psum_scatter(down_part[None].astype(jnp.bfloat16), 'fsdp', scatter_di...  94.1 us
    reduce_scatter x1, waiting for transfers between devices, shards(): lax.psum_scatter(gate_part[None].astype(jnp.bfloat16), 'fsdp', scatter_di...  93.9 us
    scatter-add x6, other arithmetic, collect(): return jax.ops.segment_sum(block_terms, segment_ids, num_segments=segments)  67.6 us
    dot_general x9, matrix products, blockwise(): jnp.einsum(pattern, left_side, right_side, preferred_element_type=jnp.flo...  40.4 us
    all_to_all x1, waiting for transfers between devices, shards(): lax.all_to_all(jnp.stack([down_blocks] * lax.axis_size('fsdp')), 'fsdp',...  40 us
    all_gather x1, waiting for transfers between devices, shards(): lax.all_gather(up_blocks, 'fsdp', axis=1, tiled=True)  29.4 us
    reduce_scatter x1, waiting for transfers between devices, shards(): lax.psum_scatter(input_term.astype(jnp.bfloat16), 'tensor', scatter_dimen...  20.3 us
  transfers between devices with their start and end apart: 8, of which 6 were waited for; matrix products, arithmetic and copies ran while one was open for 21% of the time, Pallas kernels for 0%

profile of v1, /device:TPU:2, one launch (start us, length us, event | category | flops | bytes accessed | tf_op | source)
XLA Modules:
  0.0 570.1 jit_solution(1698806312569440591)
XLA Ops:
  7.9 2.7 stack.2
  10.6 11.7 %all-to-all-start = ((bf16[32,1,2,128,128]{4,3,2,1,0:T(8,128)(2,1)}), bf16[32,1,2,128,128]{4,3,2,1,0:T(8,128)(2,1)}, u32[]{:S(2)}, u32[]{:S(2)}) async-start(bf16[32,1,2,128,128]{4,3,2,1,0:T(8,128)(2,1)} %stack.2), calls=%async_computation | async-start | bytes 4194304 | tf_op jit(solution)/shard_map/all_to_all | solution.py:41
  23.1 2.5 copy.31
  25.6 3.2 copy.32
  29.0 2.2 gather_fusion.1
  31.2 2.1 gather_fusion
  33.3 4.1 copy.36
  37.4 3.2 copy.37
  40.7 2.2 gather_fusion.3
  42.9 40.0 %all-to-all-done = bf16[32,1,2,128,128]{4,3,2,1,0:T(8,128)(2,1)} async-done(((bf16[32,1,2,128,128]{4,3,2,1,0:T(8,128)(2,1)}), bf16[32,1,2,128,128]{4,3,2,1,0:T(8,128)(2,1)}, u32[]{:S(2)}, u32[]{:S(2)}) %all-to-all-start) | async-done | bytes 2097184 | tf_op jit(solution)/shard_map/all_to_all | solution.py:41
  82.9 1.9 bitcast_multiply_fusion
  85.2 3.6 fusion.13
  88.8 8.9 %scatter_fusion.3 = f32[14,128,128]{2,1,0:T(8,128)S(1)} fusion(f32[14,128,128]{2,1,0:T(8,128)S(1)} %broadcast.238.clone, s32[64]{0:T(128)S(1)} %get-tuple-element.50, f32[64,128,128]{2,1,0:T(8,128)} %fusion.13), kind=kCustom, calls=%fused_computation.9 | custom fusion | flops 1048576 | bytes 12583168 | tf_op jit(solution)/shard_map/scatter-add | solution.py:14
  97.7 4.4 fusion.1
  102.2 8.8 %scatter_fusion = f32[14,128,128]{2,1,0:T(8,128)S(1)} fusion(f32[14,128,128]{2,1,0:T(8,128)S(1)} %broadcast.238.clone.1, s32[64]{0:T(128)S(1)} %get-tuple-element.52, f32[64,128,128]{2,1,0:T(8,128)} %fusion.1), kind=kCustom, calls=%fused_computation.6 | custom fusion | flops 1048576 | bytes 12583168 | tf_op jit(solution)/shard_map/scatter-add | solution.py:14
  111.0 29.4 %all-gather.5.cloned.1.call-done = bf16[1,64,128,128]{3,2,0,1:T(8,128)(2,1)} async-done(((bf16[1,2,128,128]{3,2,0,1:T(8,128)(2,1)}), bf16[1,64,128,128]{3,2,0,1:T(8,128)(2,1)}) %all-gather.5.cloned.1.call-update) | async-done | bytes 2097168 | tf_op jit(solution)/shard_map/all_gather | solution.py:39
  140.4 5.0 fusion.3
  145.4 8.8 %scatter_fusion.1 = f32[14,128,128]{2,1,0:T(8,128)S(1)} fusion(f32[14,128,128]{2,1,0:T(8,128)S(1)} %broadcast.238.clone.2, s32[64]{0:T(128)S(1)} %get-tuple-element.53, f32[64,128,128]{2,1,0:T(8,128)} %fusion.3), kind=kCustom, calls=%fused_computation.7 | custom fusion | flops 1048576 | bytes 12583168 | tf_op jit(solution)/shard_map/scatter-add | solution.py:14
  154.2 1.6 multiply_convert_fusion.3
  155.8 3.3 gather_fusion.2
  159.1 4.3 fusion.12
  163.5 2.5 broadcast.236.clone
  165.9 13.6 %scatter_fusion.2 = f32[64,128,128]{2,1,0:T(8,128)} fusion(f32[64,128,128]{2,1,0:T(8,128)} %broadcast.236.clone, s32[64]{0:T(128)S(1)} %get-tuple-element.51, f32[64,128,128]{2,1,0:T(8,128)} %fusion.12), kind=kCustom, calls=%fused_computation.8 | custom fusion | flops 1048576 | bytes 12583168 | tf_op jit(solution)/shard_map/scatter-add | solution.py:14
  179.6 3.9 convert_element_type.63
  183.7 0.8 copy-done.2
  184.5 2.2 gather_fusion.5
  186.7 2.2 gather_fusion.4
  188.9 5.2 fusion
  194.1 2.5 broadcast.236.clone.1
  196.6 13.8 %scatter_fusion.4 = f32[64,128,128]{2,1,0:T(8,128)} fusion(f32[64,128,128]{2,1,0:T(8,128)} %broadcast.236.clone.1, s32[64]{0:T(128)S(1)} %get-tuple-element.25, f32[64,128,128]{2,1,0:T(8,128)} %fusion), kind=kCustom, calls=%fused_computation.10 | custom fusion | flops 1048576 | bytes 12583168 | tf_op jit(solution)/shard_map/scatter-add | solution.py:14
  210.4 5.2 fusion.2
  215.6 2.5 broadcast.236.clone.2
  218.1 13.7 %scatter_fusion.5 = f32[64,128,128]{2,1,0:T(8,128)} fusion(f32[64,128,128]{2,1,0:T(8,128)} %broadcast.236.clone.2, s32[64]{0:T(128)S(1)} %get-tuple-element.19, f32[64,128,128]{2,1,0:T(8,128)} %fusion.2), kind=kCustom, calls=%fused_computation.11 | custom fusion | flops 1048576 | bytes 12583168 | tf_op jit(solution)/shard_map/scatter-add | solution.py:14
  231.8 5.8 %add_convert_fusion = bf16[64,128,128]{2,1,0:T(8,128)(2,1)} fusion(f32[64,128,128]{2,1,0:T(8,128)} %scatter_fusion.4, f32[64,128,128]{2,1,0:T(8,128)} %scatter_fusion.5), kind=kLoop, calls=%fused_computation.15 | loop fusion | flops 2097152 | bytes 10485760 | tf_op jit(solution)/shard_map/convert_element_type | solution.py:92
  237.7 1.5 copy-done.5
  239.2 4.2 fusion.5
  243.4 1.5 copy-done.7
  244.9 4.3 fusion.4
  249.3 1.5 copy-done.9
  250.8 4.2 fusion.6
  255.1 1.1 copy.35
  256.2 0.9 copy.42
  257.1 20.3 %reduce-scatter.8.cloned.1.call-done = bf16[8,128,128]{2,1,0:T(8,128)(2,1)} async-done(((bf16[64,128,128]{2,1,0:T(8,128)(2,1)}), bf16[8,128,128]{2,1,0:T(8,128)(2,1)}) %reduce-scatter.8.cloned.1.call-update) | async-done | bytes 262160 | tf_op jit(solution)/shard_map/reduce_scatter | solution.py:91
  277.3 1.1 copy.38
  278.5 0.9 copy.43
  279.3 95.9 %reduce-scatter.12.cloned.1.call-done = bf16[1,2,128,128]{3,2,1,0:T(8,128)(2,1)} async-done(((bf16[1,64,128,128]{3,2,1,0:T(8,128)(2,1)}), bf16[1,2,128,128]{3,2,1,0:T(8,128)(2,1)}) %reduce-scatter.12.cloned.1.call-update) | async-done | bytes 65552 | tf_op jit(solution)/shard_map/reduce_scatter | solution.py:84
  375.2 93.9 %reduce-scatter.10.cloned.1.call-done = bf16[1,2,128,128]{3,2,1,0:T(8,128)(2,1)} async-done(((bf16[1,64,128,128]{3,2,1,0:T(8,128)(2,1)}), bf16[1,2,128,128]{3,2,1,0:T(8,128)(2,1)}) %reduce-scatter.10.cloned.1.call-update) | async-done | bytes 65552 | tf_op jit(solution)/shard_map/reduce_scatter | solution.py:81
  469.1 94.1 %reduce-scatter.14.cloned.1.call-done = bf16[1,2,128,128]{3,2,1,0:T(8,128)(2,1)} async-done(((bf16[1,64,128,128]{3,2,1,0:T(8,128)(2,1)}), bf16[1,2,128,128]{3,2,1,0:T(8,128)(2,1)}) %reduce-scatter.14.cloned.1.call-update) | async-done | bytes 65552 | tf_op jit(solution)/shard_map/reduce_scatter | solution.py:87
  (57 shorter events, 2.7 us)
Async XLA Ops:
  7.2 90.6 %all-gather.3.cloned.1.call-start = ((), (), s32[]{:S(2)}) async-start(), calls=%async_computation.6 | async-start | bytes 2162688 | tf_op jit(solution)/shard_map/all_gather | solution.py:38
  10.6 12.6 %copy-start.10 = (bf16[128,8192]{1,0:T(8,128)(2,1)S(1)}, bf16[128,8192]{1,0:T(8,128)(2,1)}, u32[]{:S(2)}) copy-start(bf16[128,8192]{1,0:T(8,128)(2,1)} %param.13) | copy-start | bytes 6291460
  10.6 72.4 %all-to-all-start = ((bf16[32,1,2,128,128]{4,3,2,1,0:T(8,128)(2,1)}), bf16[32,1,2,128,128]{4,3,2,1,0:T(8,128)(2,1)}, u32[]{:S(2)}, u32[]{:S(2)}) async-start(bf16[32,1,2,128,128]{4,3,2,1,0:T(8,128)(2,1)} %stack.2), calls=%async_computation | async-start | bytes 4194304 | tf_op jit(solution)/shard_map/all_to_all | solution.py:41
  22.3 118.1 %all-gather.5.cloned.1.call-start = ((), (), s32[]{:S(2)}) async-start(), calls=%async_computation.7 | async-start | bytes 2162688 | tf_op jit(solution)/shard_map/all_gather | solution.py:39
  23.1 232.0 %reduce-scatter.6.cloned.1.call-start = ((), (), s32[]{:S(2)}) async-start(), calls=%async_computation.8 | async-start | bytes 2359296 | tf_op jit(solution)/shard_map/reduce_scatter | solution.py:63
  25.6 3.2 copy-start.11
  28.9 2.2 copy-start.12
  37.4 3.2 copy-start.13
  40.6 2.2 copy-start.14
  82.9 2.2 copy-start.8
  84.9 3.8 copy-start
  88.8 8.9 %copy-start.6 = (bf16[64,128,128]{2,1,0:T(8,128)(2,1)S(1)}, bf16[64,128,128]{2,1,0:T(8,128)(2,1)}, u32[]{:S(2)}) copy-start(bf16[64,128,128]{2,1,0:T(8,128)(2,1)} %gather_fusion) | copy-start | bytes 6291460
  155.8 3.3 copy-start.1
  183.5 1.0 copy-start.2
  183.5 93.8 %reduce-scatter.8.cloned.1.call-start = ((), (), s32[]{:S(2)}) async-start(), calls=%async_computation.9 | async-start | bytes 2359296 | tf_op jit(solution)/shard_map/reduce_scatter | solution.py:91
  186.7 2.2 copy-start.3
  196.6 13.8 %copy-start.4 = (bf16[1,64,128,128]{3,2,0,1:T(8,128)(2,1)S(1)}, bf16[1,64,128,128]{3,2,0,1:T(8,128)(2,1)}, u32[]{:S(2)}) copy-start(bf16[1,64,128,128]{3,2,0,1:T(8,128)(2,1)} %all-gather.5.cloned.1.call-done) | copy-start | bytes 6291460
  237.6 1.6 copy-start.5
  237.6 137.6 %reduce-scatter.12.cloned.1.call-start = ((), (), s32[]{:S(2)}) async-start(), calls=%async_computation.11 | async-start | bytes 2162688 | tf_op jit(solution)/shard_map/reduce_scatter | solution.py:84
  243.3 1.6 copy-start.7
  243.3 225.8 %reduce-scatter.10.cloned.1.call-start = ((), (), s32[]{:S(2)}) async-start(), calls=%async_computation.10 | async-start | bytes 2162688 | tf_op jit(solution)/shard_map/reduce_scatter | solution.py:81
  249.2 1.6 copy-start.9
  249.2 314.0 %reduce-scatter.14.cloned.1.call-start = ((), (), s32[]{:S(2)}) async-start(), calls=%async_computation.12 | async-start | bytes 2162688 | tf_op jit(solution)/shard_map/reduce_scatter | solution.py:87
Sparse Core Ops, SparseCore 0:
  10.5 73.1 all-gather.2
  86.3 54.0 all-gather.4
  183.6 39.7 reduce-scatter.5
  237.7 39.5 reduce-scatter.7
  281.6 93.5 reduce-scatter.11
  379.5 89.6 reduce-scatter.9
  473.5 89.6 reduce-scatter.13
